TPU v7x, 32 devices: a whole 2x2x4 slice. The times are simulated.
32 devices in a mesh: grp: 2 (over x), rep: 8 (over z, y), blk: 2 (over core).
Axes of the slice: x: 2, y: 2, z: 4, core: 2. Of those that a mesh axis runs over, the one named last changes fastest.
Arguments:
- factors: float32 [16, 1280, 1280], P('grp', ('blk', 'rep')), as said below
- damping: float32 [16], P('grp'), may hold values from 0.1 to 1
Outputs:
- root: float32 [16, 1280, 1280], P('grp', ('blk', 'rep'))
- inv_root: float32 [16, 1280, 1280], P('grp', ('blk', 'rep'))
Inputs may be any that keep to these rules, and one draw needn't show every extreme that they name: `factors`: every factor is symmetric positive semidefinite.
All inputs are finite; a program needn't handle non-finite values.
Results may differ from a plain program's by a relative error of at most 0.0035.
The roundings to bfloat16 on the way count: a program that leaves them out, or rounds other values in their place, can miss the bound.
Values may be sent and summed in bfloat16 or wider, within the bound.
No kernel may reach another device: no remote copies, remote signals or barrier semaphores. Data moves between devices by JAX's collectives and lax.ppermute only.
A program may use at most 128 MiB of HBM per device.

v0:
```python
import jax
import jax.numpy as jnp
from jax import lax
from jax.sharding import PartitionSpec as P

ITERS = 4


def per_device(factors, damping):
    fac_grp, row_count, order_full = factors.shape
    rep_count = lax.axis_size("rep")
    fac_rep = fac_grp // rep_count
    blk_rows = row_count * rep_count
    blk_idx = lax.axis_index("blk")
    rep_idx = lax.axis_index("rep")
    col_ids = lax.iota(jnp.int32, order_full)
    row_ids = blk_idx * blk_rows + rep_idx * row_count + lax.iota(jnp.int32, row_count)
    eye_block = (row_ids[:, None] == col_ids[None, :]).astype(jnp.float32)
    damped = factors + damping[:, None, None] * eye_block[None, :, :]
    factor_norms = jnp.sqrt(lax.psum(jnp.sum(damped * damped, axis=(1, 2)), ("rep", "blk")))
    scaled = (damped / factor_norms[:, None, None]).astype(jnp.bfloat16)
    scaled = scaled.reshape(rep_count, fac_rep, row_count, order_full)
    own = lax.all_to_all(scaled, "rep", split_axis=0, concat_axis=0, tiled=True)
    iterate = jnp.swapaxes(own, 0, 1).reshape(fac_rep, blk_rows, order_full)
    iter_rows = blk_idx * blk_rows + lax.iota(jnp.int32, blk_rows)
    eye_rows = (iter_rows[:, None] == col_ids[None, :]).astype(jnp.float32)[None]
    swap = ((0, 1), (1, 0))

    def own_cols(mat):
        return lax.dynamic_slice_in_dim(mat, blk_idx * blk_rows, blk_rows, 2)

    def peer_cols(mat):
        return lax.dynamic_slice_in_dim(mat, (1 - blk_idx) * blk_rows, blk_rows, 2)

    def rows_times(left, right_rows):
        peer_rows = lax.ppermute(right_rows, "blk", swap)
        first = jnp.einsum(
            "fik,fkj->fij", own_cols(left), right_rows, preferred_element_type=jnp.float32
        )
        second = jnp.einsum(
            "fik,fkj->fij", peer_cols(left), peer_rows, preferred_element_type=jnp.float32
        )
        return first + second

    step_rows = ((3.0 * eye_rows - iterate.astype(jnp.float32)) * 0.5).astype(jnp.bfloat16)
    iterate = rows_times(iterate, step_rows).astype(jnp.bfloat16)
    inverse = step_rows
    for sweep_idx in range(1, ITERS):
        moment = rows_times(inverse, iterate)
        step_rows = ((3.0 * eye_rows - moment) * 0.5).astype(jnp.bfloat16)
        both = jnp.concatenate([iterate, inverse], axis=1)
        both = rows_times(both, step_rows).astype(jnp.bfloat16)
        iterate, inverse = (both[:, :blk_rows], both[:, blk_rows:])

    def send_back(mat):
        blocks = mat.reshape(fac_rep, rep_count, row_count, order_full)
        blocks = jnp.swapaxes(blocks, 0, 1)
        back = lax.all_to_all(blocks, "rep", split_axis=0, concat_axis=0, tiled=True)
        return back.reshape(fac_grp, row_count, order_full).astype(jnp.float32)

    root_scale = jnp.sqrt(factor_norms)[:, None, None]
    return (send_back(iterate) * root_scale, send_back(inverse) / root_scale)


def solution(mesh):
    return jax.shard_map(
        per_device,
        mesh=mesh,
        in_specs=(P("grp", ("blk", "rep"), None), P("grp")),
        out_specs=(P("grp", ("blk", "rep"), None), P("grp", ("blk", "rep"), None)),
        check_vma=False,
    )
```

profile of v0, /device:TPU:0, one launch (start us, length us, event | category | flops | bytes accessed | tf_op | source)
XLA Modules:
  0.0 214.1 jit_solution(8542991458444012617)
XLA Ops:
  0.6 0.0 copy-start.2
  0.6 0.0 copy-start
  0.7 0.1 fusion.62
  0.8 0.0 copy-start.1
  0.8 0.7 copy-done.1
  1.5 2.8 %multiply_reduce_fusion = f32[8]{0:T(128)S(1)} fusion(f32[8,80,1280]{2,1,0:T(8,128)} %param.2, f32[80,1280]{1,0:T(8,128)S(1)} %fusion.62, f32[8]{0:T(128)} %param.3), kind=kLoop, calls=%fused_computation.31 | loop fusion | flops 3276792 | bytes 3686464 | tf_op jit(solution)/shard_map/reduce_sum | solution.py:20
  4.4 34.9 %psum.7 = f32[8]{0:T(128)S(1)} all-reduce(f32[8]{0:T(128)S(1)} %multiply_reduce_fusion), channel_id=1, replica_groups=mesh['grp'=2,'rep'=8,'blk'=2] {'rep','blk'}, use_global_device_ids=true, to_apply=%region_1.0 | all-reduce | flops 8 | bytes 64 | tf_op jit(solution)/shard_map/psum | solution.py:20
  39.3 0.0 copy-done.2
  39.3 0.0 copy-done
  39.3 2.7 %fusion.44 = bf16[8,1,80,1280]{3,2,1,0:T(8,128)(2,1)} fusion(f32[8]{0:T(128)S(1)} %get-tuple-element.11, f32[8,80,1280]{2,1,0:T(8,128)S(1)} %copy-done, f32[80,1280]{1,0:T(8,128)} %copy-done.1, f32[8]{0:T(128)S(1)} %copy-done.2), kind=kLoop, calls=%fused_computation.65 | loop fusion | flops 3276800 | bytes 5324864 | tf_op jit(solution)/shard_map/reshape | solution.py:22
  42.0 3.6 %all-to-all-start = ((bf16[8,1,80,1280]{3,2,1,0:T(8,128)(2,1)}), bf16[8,1,80,1280]{3,2,1,0:T(8,128)(2,1)S(1)}, u32[]{:S(2)}, u32[]{:S(2)}) async-start(bf16[8,1,80,1280]{3,2,1,0:T(8,128)(2,1)} %fusion.44), calls=%async_computation | async-start | bytes 3276800 | tf_op jit(solution)/shard_map/all_to_all | solution.py:23
  45.6 36.3 %all-to-all-done = bf16[8,1,80,1280]{3,2,1,0:T(8,128)(2,1)S(1)} async-done(((bf16[8,1,80,1280]{3,2,1,0:T(8,128)(2,1)}), bf16[8,1,80,1280]{3,2,1,0:T(8,128)(2,1)S(1)}, u32[]{:S(2)}, u32[]{:S(2)}) %all-to-all-start) | async-done | bytes 1638432 | tf_op jit(solution)/shard_map/all_to_all | solution.py:23
  81.9 0.7 multiply_convert_fusion
  82.7 0.1 collective-permute-start
  82.8 1.6 fusion.14
  84.4 2.0 collective-permute-done
  86.4 2.9 %fusion.12 = bf16[640,1280]{1,0:T(8,128)(2,1)S(1)} fusion(f32[640,1280]{1,0:T(8,128)S(1)} %fusion.14, bf16[1,640,1280]{2,1,0:T(8,128)(2,1)} %collective-permute-done, bf16[1,640,1280]{2,1,0:T(8,128)(2,1)S(1)} %bitcast.94, s32[]{:T(128)S(6)} %select_n.5), kind=kOutput, calls=%fused_computation.36 | convolution fusion | flops 1050214400 | bytes 7372804 | tf_op jit(solution)/shard_map/fik,fkj->fij/dot_general | solution.py:40
  89.3 0.2 collective-permute-start.1
  89.5 1.4 fusion.50
  91.0 1.9 collective-permute-done.1
  92.9 1.6 fusion.11
  94.5 0.2 collective-permute-start.2
  94.7 2.7 %fusion.21 = f32[1280,1280]{1,0:T(8,128)S(1)} fusion(bf16[640,1280]{1,0:T(8,128)(2,1)S(1)} %fusion.11, s32[]{:T(128)S(6)} %select_n.4, bf16[1,640,1280]{2,1,0:T(8,128)(2,1)S(1)} %bitcast.102, bf16[1,640,1280]{2,1,0:T(8,128)(2,1)S(1)} %multiply_convert_fusion), kind=kOutput, calls=%fused_computation.43 | convolution fusion | flops 2100428800 | bytes 11468804 | tf_op jit(solution)/shard_map/fik,fkj->fij/dot_general | solution.py:37
  97.5 0.6 collective-permute-done.2
  98.1 4.1 %fusion = bf16[1280,1280]{1,0:T(8,128)(2,1)S(1)} fusion(f32[1280,1280]{1,0:T(8,128)S(1)} %fusion.21, s32[]{:T(128)S(6)} %select_n.5, bf16[1,640,1280]{2,1,0:T(8,128)(2,1)S(1)} %bitcast.103, bf16[1,640,1280]{2,1,0:T(8,128)(2,1)S(1)} %multiply_convert_fusion, bf16[1,640,1280]{2,1,0:T(8,128)(2,1)S(1)} %collective-permute-done.2), kind=kOutput, calls=%fused_computation.3 | convolution fusion | flops 2103705600 | bytes 14745604 | tf_op jit(solution)/shard_map/fik,fkj->fij/dot_general | solution.py:40
  102.2 0.2 fusion.86
  102.4 0.2 collective-permute-start.3
  102.6 1.4 fusion.29
  104.1 1.9 collective-permute-done.3
  106.0 1.6 fusion.10
  107.6 0.2 collective-permute-start.4
  107.8 2.7 %fusion.38 = f32[1280,1280]{1,0:T(8,128)S(1)} fusion(bf16[640,1280]{1,0:T(8,128)(2,1)S(1)} %fusion.10, bf16[1280,1280]{1,0:T(8,128)(2,1)S(1)} %fusion, s32[]{:T(128)S(6)} %select_n.4), kind=kOutput, calls=%fused_computation.59 | convolution fusion | flops 2097152000 | bytes 9830404 | tf_op jit(solution)/shard_map/fik,fkj->fij/dot_general | solution.py:37
  110.5 0.7 collective-permute-done.4
  111.2 3.0 %fusion.1 = bf16[1280,1280]{1,0:T(8,128)(2,1)S(1)} fusion(f32[1280,1280]{1,0:T(8,128)S(1)} %fusion.38, bf16[1,640,1280]{2,1,0:T(8,128)(2,1)S(1)} %collective-permute-done.4, bf16[1280,1280]{1,0:T(8,128)(2,1)S(1)} %fusion, s32[]{:T(128)S(6)} %select_n.5), kind=kOutput, calls=%fused_computation.4 | convolution fusion | flops 2100428800 | bytes 13107204 | tf_op jit(solution)/shard_map/fik,fkj->fij/dot_general | solution.py:40
  114.2 0.2 fusion.85
  114.4 0.1 collective-permute-start.5
  114.5 1.4 fusion.25
  116.0 2.0 collective-permute-done.5
  118.0 1.6 fusion.9
  119.6 0.2 collective-permute-start.6
  119.8 2.7 %fusion.35 = f32[1280,1280]{1,0:T(8,128)S(1)} fusion(bf16[640,1280]{1,0:T(8,128)(2,1)S(1)} %fusion.9, bf16[1280,1280]{1,0:T(8,128)(2,1)S(1)} %fusion.1, s32[]{:T(128)S(6)} %select_n.4), kind=kOutput, calls=%fused_computation.56 | convolution fusion | flops 2097152000 | bytes 9830404 | tf_op jit(solution)/shard_map/fik,fkj->fij/dot_general | solution.py:37
  122.5 0.6 collective-permute-done.6
  123.2 3.0 %fusion.3 = bf16[1,1280,1280]{2,1,0:T(8,128)(2,1)S(1)} fusion(f32[1280,1280]{1,0:T(8,128)S(1)} %fusion.35, bf16[1,640,1280]{2,1,0:T(8,128)(2,1)S(1)} %collective-permute-done.6, bf16[1280,1280]{1,0:T(8,128)(2,1)S(1)} %fusion.1, s32[]{:T(128)S(6)} %select_n.5), kind=kOutput, calls=%fused_computation.6 | convolution fusion | flops 2100428800 | bytes 13107204 | tf_op jit(solution)/shard_map/fik,fkj->fij/dot_general | solution.py:40
  126.2 0.2 fusion.84
  126.4 42.4 %all_to_all.15 = bf16[8,1,80,1280]{3,2,1,0:T(8,128)(2,1)S(1)} all-to-all(bf16[8,1,80,1280]{3,2,1,0:T(8,128)(2,1)S(1)} %bitcast.96), channel_id=1, replica_groups=mesh['grp'=2,'rep'=8,'blk'=2] {'rep'}, dimensions={0} | all-to-all | bytes 3276800 | tf_op jit(solution)/shard_map/all_to_all | solution.py:58
  168.8 41.8 %all_to_all.16 = bf16[8,1,80,1280]{3,2,1,0:T(8,128)(2,1)S(1)} all-to-all(bf16[8,1,80,1280]{3,2,1,0:T(8,128)(2,1)S(1)} %bitcast.95), channel_id=1, replica_groups=mesh['grp'=2,'rep'=8,'blk'=2] {'rep'}, dimensions={0} | all-to-all | bytes 3276800 | tf_op jit(solution)/shard_map/all_to_all | solution.py:58
  210.6 3.5 %convert_divide_fusion = (f32[8,80,1280]{2,1,0:T(8,128)}, f32[8,80,1280]{2,1,0:T(8,128)}) fusion(bf16[8,1,80,1280]{3,2,1,0:T(8,128)(2,1)S(1)} %all_to_all.16, f32[8]{0:T(128)S(1)} %get-tuple-element.10, bf16[8,1,80,1280]{3,2,1,0:T(8,128)(2,1)S(1)} %all_to_all.15), kind=kLoop, calls=%fused_computation.21 | loop fusion | flops 3276800 | bytes 9830432 | tf_op jit(solution)/shard_map/div | solution.py:62
  (3 shorter events, 0.0 us)
Async XLA Ops:
  0.6 38.7 %copy-start.2 = (f32[8]{0:T(128)S(1)}, f32[8]{0:T(128)}, u32[]{:S(2)}) copy-start(f32[8]{0:T(128)} %param.3) | copy-start | bytes 100
  0.6 38.7 %copy-start = (f32[8,80,1280]{2,1,0:T(8,128)S(1)}, f32[8,80,1280]{2,1,0:T(8,128)}, u32[]{:S(2)}) copy-start(f32[8,80,1280]{2,1,0:T(8,128)} %param.2) | copy-start | bytes 9830404
  0.8 0.8 copy-start.1
  42.0 39.9 %all-to-all-start = ((bf16[8,1,80,1280]{3,2,1,0:T(8,128)(2,1)}), bf16[8,1,80,1280]{3,2,1,0:T(8,128)(2,1)S(1)}, u32[]{:S(2)}, u32[]{:S(2)}) async-start(bf16[8,1,80,1280]{3,2,1,0:T(8,128)(2,1)} %fusion.44), calls=%async_computation | async-start | bytes 3276800 | tf_op jit(solution)/shard_map/all_to_all | solution.py:23
  82.7 3.7 %collective-permute-start = (bf16[1,640,1280]{2,1,0:T(8,128)(2,1)S(1)}, bf16[1,640,1280]{2,1,0:T(8,128)(2,1)}, u32[]{:S(2)}, u32[]{:S(2)}) collective-permute-start(bf16[1,640,1280]{2,1,0:T(8,128)(2,1)S(1)} %multiply_convert_fusion), channel_id=1, source_target_pairs={{0,1},{1,0},{2,3},{3,2},{4,5},{5,4},{6,7},{7,6},{8,9},{9,8},{10,11... | collective-permute-start | bytes 4915208 | tf_op jit(solution)/shard_map/ppermute | solution.py:36
  89.3 3.6 %collective-permute-start.1 = (bf16[1,640,1280]{2,1,0:T(8,128)(2,1)S(1)}, bf16[1,640,1280]{2,1,0:T(8,128)(2,1)S(1)}, u32[]{:S(2)}, u32[]{:S(2)}) collective-permute-start(bf16[1,640,1280]{2,1,0:T(8,128)(2,1)S(1)} %bitcast.101), channel_id=1, source_target_pairs={{0,1},{1,0},{2,3},{3,2},{4,5},{5,4},{6,7},{7,6},{8,9},{9,8},{10,11... | collective-permute-start | bytes 4915208 | tf_op jit(solution)/shard_map/ppermute | solution.py:36
  94.5 3.6 %collective-permute-start.2 = (bf16[1,640,1280]{2,1,0:T(8,128)(2,1)S(1)}, bf16[1,640,1280]{2,1,0:T(8,128)(2,1)S(1)}, u32[]{:S(2)}, u32[]{:S(2)}) collective-permute-start(bf16[1,640,1280]{2,1,0:T(8,128)(2,1)S(1)} %bitcast.106), channel_id=1, source_target_pairs={{0,1},{1,0},{2,3},{3,2},{4,5},{5,4},{6,7},{7,6},{8,9},{9,8},{10,11... | collective-permute-start | bytes 4915208 | tf_op jit(solution)/shard_map/ppermute | solution.py:36
  102.4 3.6 %collective-permute-start.3 = (bf16[1,640,1280]{2,1,0:T(8,128)(2,1)S(1)}, bf16[1,640,1280]{2,1,0:T(8,128)(2,1)S(1)}, u32[]{:S(2)}, u32[]{:S(2)}) collective-permute-start(bf16[1,640,1280]{2,1,0:T(8,128)(2,1)S(1)} %get-tuple-element.6), channel_id=1, source_target_pairs={{0,1},{1,0},{2,3},{3,2},{4,5},{5,4},{6,7},{7,6},{8,9},{9,8},{10,11... | collective-permute-start | bytes 4915208 | tf_op jit(solution)/shard_map/ppermute | solution.py:36
  107.6 3.6 %collective-permute-start.4 = (bf16[1,640,1280]{2,1,0:T(8,128)(2,1)S(1)}, bf16[1,640,1280]{2,1,0:T(8,128)(2,1)S(1)}, u32[]{:S(2)}, u32[]{:S(2)}) collective-permute-start(bf16[1,640,1280]{2,1,0:T(8,128)(2,1)S(1)} %bitcast.105), channel_id=1, source_target_pairs={{0,1},{1,0},{2,3},{3,2},{4,5},{5,4},{6,7},{7,6},{8,9},{9,8},{10,11... | collective-permute-start | bytes 4915208 | tf_op jit(solution)/shard_map/ppermute | solution.py:36
  114.4 3.6 %collective-permute-start.5 = (bf16[1,640,1280]{2,1,0:T(8,128)(2,1)S(1)}, bf16[1,640,1280]{2,1,0:T(8,128)(2,1)S(1)}, u32[]{:S(2)}, u32[]{:S(2)}) collective-permute-start(bf16[1,640,1280]{2,1,0:T(8,128)(2,1)S(1)} %get-tuple-element.4), channel_id=1, source_target_pairs={{0,1},{1,0},{2,3},{3,2},{4,5},{5,4},{6,7},{7,6},{8,9},{9,8},{10,11... | collective-permute-start | bytes 4915208 | tf_op jit(solution)/shard_map/ppermute | solution.py:36
  119.6 3.6 %collective-permute-start.6 = (bf16[1,640,1280]{2,1,0:T(8,128)(2,1)S(1)}, bf16[1,640,1280]{2,1,0:T(8,128)(2,1)S(1)}, u32[]{:S(2)}, u32[]{:S(2)}) collective-permute-start(bf16[1,640,1280]{2,1,0:T(8,128)(2,1)S(1)} %bitcast.104), channel_id=1, source_target_pairs={{0,1},{1,0},{2,3},{3,2},{4,5},{5,4},{6,7},{7,6},{8,9},{9,8},{10,11... | collective-permute-start | bytes 4915208 | tf_op jit(solution)/shard_map/ppermute | solution.py:36
where the time goes:
time: 214 us
  blocking collectives  119 us (56%)
  waiting for transfers between devices  46.1 us (22%)
  matrix products  32 us (15%)
  other arithmetic  9.91 us (5%)
  starting transfers between devices  4.79 us (2%)
    all_to_all x2, blocking collectives, send_back(): lax.all_to_all(blocks, 'rep', split_axis=0, concat_axis=0, tiled=True)  84.2 us
    all_to_all x1, waiting for transfers between devices, per_device(): own = lax.all_to_all(scaled, 'rep', split_axis=0, concat_axis=0, tiled=True)  36.3 us
    psum x1, blocking collectives, per_device(): lax.psum(jnp.sum(damped * damped, axis=(1, 2)), ('rep', 'blk'))  34.9 us
    dot_general x7, matrix products, rows_times(): jnp.einsum('fik,fkj->fij', peer_cols(left), peer_rows, preferred_element_...  17.9 us
    dot_general x7, matrix products, rows_times(): jnp.einsum('fik,fkj->fij', own_cols(left), right_rows, preferred_element_...  14.1 us
    ppermute x7, waiting for transfers between devices, rows_times(): peer_rows = lax.ppermute(right_rows, 'blk', swap)  9.73 us
  transfers between devices with their start and end apart: 8, of which 8 were waited for; matrix products, arithmetic and copies ran while one was open for 7% of the time, Pallas kernels for 0%

commit v1 on v0

--- a/solution.py
+++ b/solution.py
@@ -17,7 +17,9 @@
     row_ids = blk_idx * blk_rows + rep_idx * row_count + lax.iota(jnp.int32, row_count)
     eye_block = (row_ids[:, None] == col_ids[None, :]).astype(jnp.float32)
     damped = factors + damping[:, None, None] * eye_block[None, :, :]
-    factor_norms = jnp.sqrt(lax.psum(jnp.sum(damped * damped, axis=(1, 2)), ("rep", "blk")))
+    factor_norms = jnp.sqrt(
+        jnp.sum(lax.all_gather(jnp.sum(damped * damped, axis=(1, 2)), ("rep", "blk")), axis=0)
+    )
     scaled = (damped / factor_norms[:, None, None]).astype(jnp.bfloat16)
     scaled = scaled.reshape(rep_count, fac_rep, row_count, order_full)
     own = lax.all_to_all(scaled, "rep", split_axis=0, concat_axis=0, tiled=True)

time: 214 us -> 216 us (level)
    psum x1 -> x0, blocking collectives: 34.9 us -> none  [per_device(): lax.psum(jnp.sum(damped * damped, axis=(1, 2)), ('rep', 'blk'))]
    unnamed x0 -> x1, blocking collectives: none -> 34.9 us
where the time goes in v1:
time: 216 us
  blocking collectives  119 us (55%)
  waiting for transfers between devices  46.1 us (21%)
  matrix products  32 us (15%)
  other arithmetic  9.68 us (4%)
  starting transfers between devices  4.76 us (2%)
  local copies, waits for them, and re-layouts  2.42 us (1%)
    all_to_all x2, blocking collectives, send_back(): lax.all_to_all(blocks, 'rep', split_axis=0, concat_axis=0, tiled=True)  84.2 us
    all_to_all x1, waiting for transfers between devices, per_device(): own = lax.all_to_all(scaled, 'rep', split_axis=0, concat_axis=0, tiled=True)  36.3 us
    unnamed x1, blocking collectives  34.9 us
    dot_general x7, matrix products, rows_times(): jnp.einsum('fik,fkj->fij', peer_cols(left), peer_rows, preferred_element_...  17.9 us
    dot_general x7, matrix products, rows_times(): jnp.einsum('fik,fkj->fij', own_cols(left), right_rows, preferred_element_...  14.1 us
    ppermute x7, waiting for transfers between devices, rows_times(): peer_rows = lax.ppermute(right_rows, 'blk', swap)  9.76 us
  transfers between devices with their start and end apart: 8, of which 8 were waited for; matrix products, arithmetic and copies ran while one was open for 7% of the time, Pallas kernels for 0%

profile of v1, /device:TPU:0, one launch (start us, length us, event | category | flops | bytes accessed | tf_op | source)
XLA Modules:
  0.0 215.6 jit_solution(1518995277820651262)
XLA Ops:
  0.6 0.0 copy-start.2
  0.6 0.0 copy-start
  0.7 0.1 fusion.62
  0.8 0.0 copy-start.1
  0.8 1.5 dynamic-slice.16
  2.9 0.0 copy-done.1
  2.9 2.6 %multiply_reduce_fusion = f32[8]{0:T(128)S(1)} fusion(f32[8,80,1280]{2,1,0:T(8,128)} %param.2, f32[80,1280]{1,0:T(8,128)S(1)} %fusion.62, f32[8]{0:T(128)} %param.3), kind=kLoop, calls=%fused_computation.31 | loop fusion | flops 3276792 | bytes 3686464 | tf_op jit(solution)/shard_map/reduce_sum | solution.py:21
  5.5 0.2 dynamic-update-slice
  5.7 34.9 %all-reduce = f32[128]{0:T(128)S(1)} all-reduce(f32[128]{0:T(128)S(1)} %dynamic-update-slice), channel_id=2, replica_groups=mesh['grp'=2,'rep'=8,'blk'=2] {'rep','blk'}, use_global_device_ids=true, to_apply=%add | all-reduce | flops 128 | bytes 1024
  40.7 0.1 reshape.309
  40.8 2.7 %fusion.44 = bf16[8,1,80,1280]{3,2,1,0:T(8,128)(2,1)} fusion(f32[8]{0:T(128)S(1)} %get-tuple-element.11, f32[8,80,1280]{2,1,0:T(8,128)S(1)} %copy-done, f32[80,1280]{1,0:T(8,128)} %copy-done.1, f32[8]{0:T(128)S(1)} %copy-done.2), kind=kLoop, calls=%fused_computation.65 | loop fusion | flops 3276800 | bytes 5324864 | tf_op jit(solution)/shard_map/reshape | solution.py:24
  43.5 3.6 %all-to-all-start = ((bf16[8,1,80,1280]{3,2,1,0:T(8,128)(2,1)}), bf16[8,1,80,1280]{3,2,1,0:T(8,128)(2,1)S(1)}, u32[]{:S(2)}, u32[]{:S(2)}) async-start(bf16[8,1,80,1280]{3,2,1,0:T(8,128)(2,1)} %fusion.44), calls=%async_computation | async-start | bytes 3276800 | tf_op jit(solution)/shard_map/all_to_all | solution.py:25
  47.1 36.3 %all-to-all-done = bf16[8,1,80,1280]{3,2,1,0:T(8,128)(2,1)S(1)} async-done(((bf16[8,1,80,1280]{3,2,1,0:T(8,128)(2,1)}), bf16[8,1,80,1280]{3,2,1,0:T(8,128)(2,1)S(1)}, u32[]{:S(2)}, u32[]{:S(2)}) %all-to-all-start) | async-done | bytes 1638432 | tf_op jit(solution)/shard_map/all_to_all | solution.py:25
  83.4 0.7 multiply_convert_fusion
  84.2 0.1 collective-permute-start
  84.2 1.6 fusion.14
  85.9 2.0 collective-permute-done
  87.9 2.9 %fusion.12 = bf16[640,1280]{1,0:T(8,128)(2,1)S(1)} fusion(f32[640,1280]{1,0:T(8,128)S(1)} %fusion.14, bf16[1,640,1280]{2,1,0:T(8,128)(2,1)} %collective-permute-done, bf16[1,640,1280]{2,1,0:T(8,128)(2,1)S(1)} %bitcast.95, s32[]{:T(128)S(6)} %select_n.5), kind=kOutput, calls=%fused_computation.36 | convolution fusion | flops 1050214400 | bytes 7372804 | tf_op jit(solution)/shard_map/fik,fkj->fij/dot_general | solution.py:42
  90.8 0.2 collective-permute-start.1
  91.0 1.4 fusion.50
  92.4 1.9 collective-permute-done.1
  94.3 1.6 fusion.11
  96.0 0.2 collective-permute-start.2
  96.2 2.7 %fusion.21 = f32[1280,1280]{1,0:T(8,128)S(1)} fusion(bf16[640,1280]{1,0:T(8,128)(2,1)S(1)} %fusion.11, s32[]{:T(128)S(6)} %select_n.4, bf16[1,640,1280]{2,1,0:T(8,128)(2,1)S(1)} %bitcast.103, bf16[1,640,1280]{2,1,0:T(8,128)(2,1)S(1)} %multiply_convert_fusion), kind=kOutput, calls=%fused_computation.43 | convolution fusion | flops 2100428800 | bytes 11468804 | tf_op jit(solution)/shard_map/fik,fkj->fij/dot_general | solution.py:39
  98.9 0.6 collective-permute-done.2
  99.5 4.1 %fusion = bf16[1280,1280]{1,0:T(8,128)(2,1)S(1)} fusion(f32[1280,1280]{1,0:T(8,128)S(1)} %fusion.21, s32[]{:T(128)S(6)} %select_n.5, bf16[1,640,1280]{2,1,0:T(8,128)(2,1)S(1)} %bitcast.104, bf16[1,640,1280]{2,1,0:T(8,128)(2,1)S(1)} %multiply_convert_fusion, bf16[1,640,1280]{2,1,0:T(8,128)(2,1)S(1)} %collective-permute-done.2), kind=kOutput, calls=%fused_computation.3 | convolution fusion | flops 2103705600 | bytes 14745604 | tf_op jit(solution)/shard_map/fik,fkj->fij/dot_general | solution.py:42
  103.7 0.2 fusion.86
  103.9 0.2 collective-permute-start.3
  104.1 1.4 fusion.29
  105.5 1.9 collective-permute-done.3
  107.5 1.6 fusion.10
  109.1 0.2 collective-permute-start.4
  109.3 2.7 %fusion.38 = f32[1280,1280]{1,0:T(8,128)S(1)} fusion(bf16[640,1280]{1,0:T(8,128)(2,1)S(1)} %fusion.10, bf16[1280,1280]{1,0:T(8,128)(2,1)S(1)} %fusion, s32[]{:T(128)S(6)} %select_n.4), kind=kOutput, calls=%fused_computation.59 | convolution fusion | flops 2097152000 | bytes 9830404 | tf_op jit(solution)/shard_map/fik,fkj->fij/dot_general | solution.py:39
  112.0 0.7 collective-permute-done.4
  112.7 3.0 %fusion.1 = bf16[1280,1280]{1,0:T(8,128)(2,1)S(1)} fusion(f32[1280,1280]{1,0:T(8,128)S(1)} %fusion.38, bf16[1,640,1280]{2,1,0:T(8,128)(2,1)S(1)} %collective-permute-done.4, bf16[1280,1280]{1,0:T(8,128)(2,1)S(1)} %fusion, s32[]{:T(128)S(6)} %select_n.5), kind=kOutput, calls=%fused_computation.4 | convolution fusion | flops 2100428800 | bytes 13107204 | tf_op jit(solution)/shard_map/fik,fkj->fij/dot_general | solution.py:42
  115.7 0.2 fusion.85
  115.9 0.1 collective-permute-start.5
  116.0 1.4 fusion.25
  117.5 2.0 collective-permute-done.5
  119.4 1.6 fusion.9
  121.1 0.2 collective-permute-start.6
  121.3 2.7 %fusion.35 = f32[1280,1280]{1,0:T(8,128)S(1)} fusion(bf16[640,1280]{1,0:T(8,128)(2,1)S(1)} %fusion.9, bf16[1280,1280]{1,0:T(8,128)(2,1)S(1)} %fusion.1, s32[]{:T(128)S(6)} %select_n.4), kind=kOutput, calls=%fused_computation.56 | convolution fusion | flops 2097152000 | bytes 9830404 | tf_op jit(solution)/shard_map/fik,fkj->fij/dot_general | solution.py:39
  124.0 0.6 collective-permute-done.6
  124.7 3.0 %fusion.3 = bf16[1,1280,1280]{2,1,0:T(8,128)(2,1)S(1)} fusion(f32[1280,1280]{1,0:T(8,128)S(1)} %fusion.35, bf16[1,640,1280]{2,1,0:T(8,128)(2,1)S(1)} %collective-permute-done.6, bf16[1280,1280]{1,0:T(8,128)(2,1)S(1)} %fusion.1, s32[]{:T(128)S(6)} %select_n.5), kind=kOutput, calls=%fused_computation.6 | convolution fusion | flops 2100428800 | bytes 13107204 | tf_op jit(solution)/shard_map/fik,fkj->fij/dot_general | solution.py:42
  127.6 0.2 fusion.84
  127.9 42.4 %all_to_all.15 = bf16[8,1,80,1280]{3,2,1,0:T(8,128)(2,1)S(1)} all-to-all(bf16[8,1,80,1280]{3,2,1,0:T(8,128)(2,1)S(1)} %bitcast.97), channel_id=1, replica_groups=mesh['grp'=2,'rep'=8,'blk'=2] {'rep'}, dimensions={0} | all-to-all | bytes 3276800 | tf_op jit(solution)/shard_map/all_to_all | solution.py:60
  170.3 41.8 %all_to_all.16 = bf16[8,1,80,1280]{3,2,1,0:T(8,128)(2,1)S(1)} all-to-all(bf16[8,1,80,1280]{3,2,1,0:T(8,128)(2,1)S(1)} %bitcast.96), channel_id=1, replica_groups=mesh['grp'=2,'rep'=8,'blk'=2] {'rep'}, dimensions={0} | all-to-all | bytes 3276800 | tf_op jit(solution)/shard_map/all_to_all | solution.py:60
  212.0 3.5 %convert_divide_fusion = (f32[8,80,1280]{2,1,0:T(8,128)}, f32[8,80,1280]{2,1,0:T(8,128)}) fusion(bf16[8,1,80,1280]{3,2,1,0:T(8,128)(2,1)S(1)} %all_to_all.16, f32[8]{0:T(128)S(1)} %get-tuple-element.10, bf16[8,1,80,1280]{3,2,1,0:T(8,128)(2,1)S(1)} %all_to_all.15), kind=kLoop, calls=%fused_computation.21 | loop fusion | flops 3276800 | bytes 9830432 | tf_op jit(solution)/shard_map/div | solution.py:64
  (7 shorter events, 0.0 us)
Async XLA Ops:
  0.6 40.2 %copy-start.2 = (f32[8]{0:T(128)S(1)}, f32[8]{0:T(128)}, u32[]{:S(2)}) copy-start(f32[8]{0:T(128)} %param.3) | copy-start | bytes 100
  0.6 40.2 %copy-start = (f32[8,80,1280]{2,1,0:T(8,128)S(1)}, f32[8,80,1280]{2,1,0:T(8,128)}, u32[]{:S(2)}) copy-start(f32[8,80,1280]{2,1,0:T(8,128)} %param.2) | copy-start | bytes 9830404
  0.8 2.1 copy-start.1
  43.5 39.9 %all-to-all-start = ((bf16[8,1,80,1280]{3,2,1,0:T(8,128)(2,1)}), bf16[8,1,80,1280]{3,2,1,0:T(8,128)(2,1)S(1)}, u32[]{:S(2)}, u32[]{:S(2)}) async-start(bf16[8,1,80,1280]{3,2,1,0:T(8,128)(2,1)} %fusion.44), calls=%async_computation | async-start | bytes 3276800 | tf_op jit(solution)/shard_map/all_to_all | solution.py:25
  84.2 3.7 %collective-permute-start = (bf16[1,640,1280]{2,1,0:T(8,128)(2,1)S(1)}, bf16[1,640,1280]{2,1,0:T(8,128)(2,1)}, u32[]{:S(2)}, u32[]{:S(2)}) collective-permute-start(bf16[1,640,1280]{2,1,0:T(8,128)(2,1)S(1)} %multiply_convert_fusion), channel_id=1, source_target_pairs={{0,1},{1,0},{2,3},{3,2},{4,5},{5,4},{6,7},{7,6},{8,9},{9,8},{10,11... | collective-permute-start | bytes 4915208 | tf_op jit(solution)/shard_map/ppermute | solution.py:38
  90.8 3.6 %collective-permute-start.1 = (bf16[1,640,1280]{2,1,0:T(8,128)(2,1)S(1)}, bf16[1,640,1280]{2,1,0:T(8,128)(2,1)S(1)}, u32[]{:S(2)}, u32[]{:S(2)}) collective-permute-start(bf16[1,640,1280]{2,1,0:T(8,128)(2,1)S(1)} %bitcast.102), channel_id=1, source_target_pairs={{0,1},{1,0},{2,3},{3,2},{4,5},{5,4},{6,7},{7,6},{8,9},{9,8},{10,11... | collective-permute-start | bytes 4915208 | tf_op jit(solution)/shard_map/ppermute | solution.py:38
  96.0 3.6 %collective-permute-start.2 = (bf16[1,640,1280]{2,1,0:T(8,128)(2,1)S(1)}, bf16[1,640,1280]{2,1,0:T(8,128)(2,1)S(1)}, u32[]{:S(2)}, u32[]{:S(2)}) collective-permute-start(bf16[1,640,1280]{2,1,0:T(8,128)(2,1)S(1)} %bitcast.107), channel_id=1, source_target_pairs={{0,1},{1,0},{2,3},{3,2},{4,5},{5,4},{6,7},{7,6},{8,9},{9,8},{10,11... | collective-permute-start | bytes 4915208 | tf_op jit(solution)/shard_map/ppermute | solution.py:38
  103.9 3.6 %collective-permute-start.3 = (bf16[1,640,1280]{2,1,0:T(8,128)(2,1)S(1)}, bf16[1,640,1280]{2,1,0:T(8,128)(2,1)S(1)}, u32[]{:S(2)}, u32[]{:S(2)}) collective-permute-start(bf16[1,640,1280]{2,1,0:T(8,128)(2,1)S(1)} %get-tuple-element.6), channel_id=1, source_target_pairs={{0,1},{1,0},{2,3},{3,2},{4,5},{5,4},{6,7},{7,6},{8,9},{9,8},{10,11... | collective-permute-start | bytes 4915208 | tf_op jit(solution)/shard_map/ppermute | solution.py:38
  109.1 3.6 %collective-permute-start.4 = (bf16[1,640,1280]{2,1,0:T(8,128)(2,1)S(1)}, bf16[1,640,1280]{2,1,0:T(8,128)(2,1)S(1)}, u32[]{:S(2)}, u32[]{:S(2)}) collective-permute-start(bf16[1,640,1280]{2,1,0:T(8,128)(2,1)S(1)} %bitcast.106), channel_id=1, source_target_pairs={{0,1},{1,0},{2,3},{3,2},{4,5},{5,4},{6,7},{7,6},{8,9},{9,8},{10,11... | collective-permute-start | bytes 4915208 | tf_op jit(solution)/shard_map/ppermute | solution.py:38
  115.9 3.6 %collective-permute-start.5 = (bf16[1,640,1280]{2,1,0:T(8,128)(2,1)S(1)}, bf16[1,640,1280]{2,1,0:T(8,128)(2,1)S(1)}, u32[]{:S(2)}, u32[]{:S(2)}) collective-permute-start(bf16[1,640,1280]{2,1,0:T(8,128)(2,1)S(1)} %get-tuple-element.4), channel_id=1, source_target_pairs={{0,1},{1,0},{2,3},{3,2},{4,5},{5,4},{6,7},{7,6},{8,9},{9,8},{10,11... | collective-permute-start | bytes 4915208 | tf_op jit(solution)/shard_map/ppermute | solution.py:38
  121.1 3.6 %collective-permute-start.6 = (bf16[1,640,1280]{2,1,0:T(8,128)(2,1)S(1)}, bf16[1,640,1280]{2,1,0:T(8,128)(2,1)S(1)}, u32[]{:S(2)}, u32[]{:S(2)}) collective-permute-start(bf16[1,640,1280]{2,1,0:T(8,128)(2,1)S(1)} %bitcast.105), channel_id=1, source_target_pairs={{0,1},{1,0},{2,3},{3,2},{4,5},{5,4},{6,7},{7,6},{8,9},{9,8},{10,11... | collective-permute-start | bytes 4915208 | tf_op jit(solution)/shard_map/ppermute | solution.py:38
